TPU v7x, 256 devices: a whole 4x4x8 slice. The times are simulated.
256 devices in a mesh: row: 32 (over y, z), col: 8 (over x, core).
Axes of the slice: x: 4, y: 4, z: 8, core: 2. Of those that a mesh axis runs over, the one named last changes fastest.
Arguments:
- grams: bfloat16 [4, 3584, 3584], P(None, 'row', 'col'), as said below
- weights: bfloat16 [4, 3584, 7168], P(None, 'row', 'col'), may hold values from -6 to 6
Outputs:
- merged: float32 [3584, 7168], P('row', 'col')
- residual: float32 [3584, 7168], P('row', 'col')
Inputs may be any that keep to these rules, and one draw needn't show every extreme that they name: `grams`: each of the 4 matrices is symmetric and positive definite.
All inputs are finite; a program needn't handle non-finite values.
Results may differ from a plain program's by a relative error of at most 0.012.
The roundings to bfloat16 on the way count: a program that leaves them out, or rounds other values in their place, can miss the bound.
Values may be sent and summed in bfloat16 or wider, within the bound.
A program may use at most 256 MiB of HBM per device.

v0:
```python
import jax
import jax.numpy as jnp
from jax import lax
from jax.sharding import Mesh
from jax.sharding import PartitionSpec as P

ITERS = 2
ROW = ("row_0", "row_1")


def sum_by_axis(so_far, axes):
    for axis in axes:
        so_far = lax.psum_scatter(so_far, axis, scatter_dimension=0, tiled=True)
    return so_far


def sent_to_all(x, axis):
    copies = jnp.broadcast_to(x, (lax.axis_size(axis), *x.shape))
    return lax.all_to_all(copies, axis, split_axis=0, concat_axis=0, tiled=True)


def of_everyone(x, axis):
    return sent_to_all(x, axis).sum(axis=0)


def together(arrays, axis):
    ravelled, at, done = (jnp.concatenate([a.reshape(-1) for a in arrays]), 0, [])
    so_far = of_everyone(ravelled, axis)
    for a in arrays:
        done.append(so_far[at : at + a.size].reshape(a.shape))
        at += a.size
    return tuple(done)


def shards(grams, weights):
    slab_rows = grams.shape[1]
    col_count = weights.shape[2]
    first_row = lax.axis_index(ROW) * slab_rows
    high = lax.Precision.HIGHEST
    gram_slabs = lax.all_gather(grams, "col", axis=2, tiled=True)
    gram_total = jnp.sum(gram_slabs, axis=0, dtype=jnp.float32)
    square_block = lax.dynamic_slice_in_dim(gram_slabs, first_row, slab_rows, gram_slabs.ndim - 1)
    diag_total = jnp.einsum(
        "mr,mrc->rc",
        jnp.diagonal(square_block, axis1=-2, axis2=-1).astype(jnp.float32),
        weights.astype(jnp.float32),
    )
    product = sum_by_axis(
        jnp.einsum("mrk,mrc->kc", gram_slabs, weights, preferred_element_type=jnp.float32), ROW
    )
    right_side = 0.9 * product + 0.1 * diag_total
    total_diag = jnp.diagonal(lax.dynamic_slice_in_dim(gram_total, first_row, slab_rows, 1))
    merged = jnp.zeros((slab_rows, col_count), jnp.float32)
    residual = right_side
    direction = right_side
    for iteration in range(ITERS):
        rounded = direction.astype(jnp.bfloat16)
        shard_piece = lax.all_gather(rounded, ROW, axis=0, tiled=True)
        add_columns = lax.slice_in_dim(gram_total, 0, shard_piece.shape[0], axis=1)
        mapped = jnp.zeros((slab_rows, col_count), jnp.float32) + jnp.dot(
            add_columns, shard_piece.astype(jnp.float32), precision=high
        )
        mapped = 0.9 * mapped + 0.1 * total_diag[:, None] * rounded.astype(jnp.float32)
        curvature, cross_term, square, norm_now = together(
            (
                jnp.sum(direction * mapped, axis=0),
                jnp.sum(residual * mapped, axis=0),
                jnp.sum(mapped * mapped, axis=0),
                jnp.sum(residual * residual, axis=0),
            ),
            ROW,
        )
        step_length = norm_now / curvature
        merged = merged + step_length * direction
        residual = residual - step_length * mapped
        if iteration + 1 < ITERS:
            norm_next = (
                norm_now - 2.0 * step_length * cross_term + step_length * step_length * square
            )
            direction = residual + norm_next / norm_now * direction
    return (merged, residual)


def solution(mesh):
    torus = Mesh(mesh.devices.reshape(4, 8, mesh.shape["col"]), ("row_0", "row_1", "col"))
    in_specs = (P(None, ROW, "col"), P(None, ROW, "col"))
    out_specs = (P(ROW, "col"), P(ROW, "col"))
    return jax.shard_map(
        shards, mesh=torus, in_specs=in_specs, out_specs=out_specs, check_vma=False
    )
```

profile of v0, /device:TPU:32, one launch (start us, length us, event | category | flops | bytes accessed | tf_op | source)
XLA Modules:
  0.0 467.3 jit_solution(11836406161750740182)
XLA Ops:
  7.2 0.0 all-gather.4.cloned.1.call-start
  7.2 2.1 copy.14
  9.3 0.0 all-gather.4.cloned.1.call-update
  9.3 0.0 reduce-scatter.3.cloned.1.call-start
  9.4 35.5 %all-gather.4.cloned.1.call-done = bf16[4,112,3584]{1,2,0:T(8,128)(2,1)} async-done(((bf16[4,112,448]{1,2,0:T(8,128)(2,1)}), bf16[4,112,3584]{1,2,0:T(8,128)(2,1)}) %all-gather.4.cloned.1.call-update) | async-done | bytes 3211280 | tf_op jit(solution)/shard_map/all_gather | solution.py:40
  44.9 8.9 %convolution_bitcast_fusion = f32[3584,896]{1,0:T(8,128)} fusion(bf16[4,112,3584]{1,2,0:T(8,128)(2,1)} %all-gather.4.cloned.1.call-done, bf16[4,112,896]{2,1,0:T(8,128)(2,1)S(1)} %copy-done), kind=kOutput, calls=%fused_computation.2 | convolution fusion | flops 2877292544 | bytes 16859136 | tf_op jit(solution)/shard_map/mrk,mrc->kc/dot_general | solution.py:49
  53.7 0.0 reduce-scatter.3.cloned.1.call-update
  53.8 0.0 reduce-scatter.5.cloned.1.call-start
  53.8 119.3 %reduce-scatter.3.cloned.1.call-done = f32[896,896]{1,0:T(8,128)} async-done(((f32[3584,896]{1,0:T(8,128)}), f32[896,896]{1,0:T(8,128)}) %reduce-scatter.3.cloned.1.call-update) | async-done | bytes 3211280 | tf_op jit(solution)/shard_map/reduce_scatter | solution.py:13
  173.1 0.0 all-gather.6.cloned.1.call-start
  173.2 0.9 constant_dynamic-slice_fusion.1
  174.1 3.2 copy.15
  177.3 2.9 gather_fusion
  180.2 0.6 fusion.2
  180.8 41.3 %reduce-scatter.5.cloned.1.call-done = f32[112,896]{1,0:T(8,128)} async-done(((f32[896,896]{1,0:T(8,128)}), f32[112,896]{1,0:T(8,128)}) %reduce-scatter.5.cloned.1.call-update) | async-done | bytes 401424 | tf_op jit(solution)/shard_map/reduce_scatter | solution.py:13
  222.1 1.8 fusion.10
  223.9 0.0 all-gather.8.cloned.1.call-start
  223.9 3.0 convert_reduce_fusion
  227.0 0.1 copy.24
  227.1 1.7 gather_fusion.1
  228.8 85.2 %all-gather.6.cloned.1.call-done = bf16[3584,896]{1,0:T(8,128)(2,1)} async-done(((bf16[112,896]{1,0:T(8,128)(2,1)}), bf16[3584,896]{1,0:T(8,128)(2,1)}) %all-gather.6.cloned.1.call-update) | async-done | bytes 6422544 | tf_op jit(solution)/shard_map/all_gather | solution.py:58
  314.0 7.0 %multiply_reduce_fusion.6 = (f32[896]{0:T(1024)S(1)}, f32[896]{0:T(1024)S(1)}, f32[896]{0:T(1024)S(1)}, f32[112,896]{1,0:T(8,128)}) fusion(f32[112,896]{1,0:T(8,128)S(1)} %get-tuple-element.14, bf16[112,896]{1,0:T(8,128)(2,1)S(1)} %copy-done.1, f32[112]{0:T(128)S(1)} %broadcast_multiply_fusion, f32[112,3584]{0,1:T(8,128)S(1)} %convert_reduce_fusion, ...), kind=kOutput, calls=%fused_computation.22 | convolution fusion | flops 4316939776 | bytes 9042880 | tf_op jit(solution)/shard_map/dot_general | solution.py:60
  320.9 0.2 broadcast_in_dim.12
  321.2 21.5 %all_to_all.12 = f32[32,1,3584]{2,1,0:T(1,128)S(1)} all-to-all(f32[32,1,3584]{2,1,0:T(1,128)S(1)} %broadcast_in_dim.12), channel_id=1, replica_groups=mesh['row_0'=4,'row_1'=8,'col'=8] {'row_0','row_1'}, dimensions={0} | all-to-all | bytes 917504 | tf_op jit(solution)/shard_map/all_to_all | solution.py:19
  342.7 0.3 reduce_sum.98
  343.0 1.7 fusion.5
  344.8 84.9 %all-gather.8.cloned.1.call-done = bf16[3584,896]{1,0:T(8,128)(2,1)} async-done(((bf16[112,896]{1,0:T(8,128)(2,1)}), bf16[3584,896]{1,0:T(8,128)(2,1)}) %all-gather.8.cloned.1.call-update) | async-done | bytes 6422544 | tf_op jit(solution)/shard_map/all_gather | solution.py:58
  429.7 7.0 %multiply_reduce_fusion.3 = (f32[896]{0:T(1024)S(1)}, f32[896]{0:T(1024)S(1)}, f32[896]{0:T(1024)S(1)}, f32[896]{0:T(1024)S(1)}, f32[112,896]{1,0:T(8,128)}) fusion(f32[112,896]{1,0:T(8,128)S(1)} %get-tuple-element.10, f32[112,896]{1,0:T(8,128)S(1)} %get-tuple-element.14, f32[896]{0:T(1024)S(1)} %get-tuple-element.11, ...), kind=kOutput, calls=%fused_computation.17 | convolution fusion | flops 4317340160 | bytes 9451456 | tf_op jit(solution)/shard_map/dot_general | solution.py:60
  436.7 0.2 broadcast_in_dim.13
  437.0 21.5 %all_to_all.13 = f32[32,1,3584]{2,1,0:T(1,128)S(1)} all-to-all(f32[32,1,3584]{2,1,0:T(1,128)S(1)} %broadcast_in_dim.13), channel_id=1, replica_groups=mesh['row_0'=4,'row_1'=8,'col'=8] {'row_0','row_1'}, dimensions={0} | all-to-all | bytes 917504 | tf_op jit(solution)/shard_map/all_to_all | solution.py:19
  458.5 0.3 reduce_sum.103
  458.8 2.0 multiply_subtract_fusion
  (14 shorter events, 0.1 us)
Async XLA Ops:
  7.2 37.7 %copy-start = (bf16[4,112,896]{2,1,0:T(8,128)(2,1)S(1)}, bf16[4,112,896]{2,1,0:T(8,128)(2,1)}, u32[]{:S(2)}) copy-start(bf16[4,112,896]{2,1,0:T(8,128)(2,1)} %param.3) | copy-start | bytes 2408452
  7.2 37.7 %all-gather.4.cloned.1.call-start = ((), (), s32[]{:S(2)}) async-start(), calls=%async_computation.4 | async-start | bytes 4128768 | tf_op jit(solution)/shard_map/all_gather | solution.py:40
  9.3 163.8 %reduce-scatter.3.cloned.1.call-start = ((), (), s32[]{:S(2)}) async-start(), calls=%async_computation.5 | async-start | bytes 16056320 | tf_op jit(solution)/shard_map/reduce_scatter | solution.py:13
  53.8 168.3 %reduce-scatter.5.cloned.1.call-start = ((), (), s32[]{:S(2)}) async-start(), calls=%async_computation.6 | async-start | bytes 3612672 | tf_op jit(solution)/shard_map/reduce_scatter | solution.py:13
  173.1 140.9 %all-gather.6.cloned.1.call-start = ((), (), s32[]{:S(2)}) async-start(), calls=%async_computation.7 | async-start | bytes 6623232 | tf_op jit(solution)/shard_map/all_gather | solution.py:58
  223.9 90.1 %copy-start.1 = (bf16[112,896]{1,0:T(8,128)(2,1)S(1)}, bf16[112,896]{1,0:T(8,128)(2,1)}, u32[]{:S(2)}) copy-start(bf16[112,896]{1,0:T(8,128)(2,1)} %get-tuple-element.13) | copy-start | bytes 602116
  223.9 205.8 %all-gather.8.cloned.1.call-start = ((), (), s32[]{:S(2)}) async-start(), calls=%async_computation.8 | async-start | bytes 6623232 | tf_op jit(solution)/shard_map/all_gather | solution.py:58
Sparse Core Ops, SparseCore 0:
  9.8 34.9 all-gather.3
  53.9 119.1 reduce-scatter.2
  175.6 46.4 reduce-scatter.4
  225.1 88.8 all-gather.5
  344.9 84.7 all-gather.7
where the time goes:
time: 468 us; the launch traced here: 467 us
  waiting for transfers between devices  366 us (78%)
  blocking collectives  43.1 us (9%)
  matrix products  23.4 us (5%)
  between operations  13.9 us (3%)
  local copies, waits for them, and re-layouts  11.4 us (2%)
  other arithmetic  9.11 us (2%)
    all_gather x2, waiting for transfers between devices, shards(): shard_piece = lax.all_gather(rounded, ROW, axis=0, tiled=True)  170 us
    reduce_scatter x2, waiting for transfers between devices, sum_by_axis(): so_far = lax.psum_scatter(so_far, axis, scatter_dimension=0, tiled=True)  161 us
    all_to_all x2, blocking collectives, sent_to_all(): return lax.all_to_all(copies, axis, split_axis=0, concat_axis=0, tiled=True)  43.1 us
    all_gather x1, waiting for transfers between devices, shards(): gram_slabs = lax.all_gather(grams, 'col', axis=2, tiled=True)  35.5 us
    dot_general x2, matrix products, shards(): jnp.dot(add_columns, shard_piece.astype(jnp.float32), precision=high)  14 us
  transfers between devices with their start and end apart: 5, of which 5 were waited for; matrix products, arithmetic and copies ran while one was open for 3% of the time, Pallas kernels for 0%

commit v1 on v0

--- a/solution.py
+++ b/solution.py
@@ -55,7 +55,8 @@
     direction = right_side
     for iteration in range(ITERS):
         rounded = direction.astype(jnp.bfloat16)
-        shard_piece = lax.all_gather(rounded, ROW, axis=0, tiled=True)
+        outgoing = jnp.stack([rounded] * lax.axis_size(ROW))
+        shard_piece = jnp.concatenate(lax.all_to_all(outgoing, ROW, 0, 0), axis=0)
         add_columns = lax.slice_in_dim(gram_total, 0, shard_piece.shape[0], axis=1)
         mapped = jnp.zeros((slab_rows, col_count), jnp.float32) + jnp.dot(
             add_columns, shard_piece.astype(jnp.float32), precision=high

time: 468 us -> 591 us (1.26)
  blocking collectives: 43.1 us -> 192 us
  waiting for transfers between devices: 366 us -> 332 us
  starting transfers between devices: 0.2 us -> 9.08 us
    all_gather x2 -> x0, waiting for transfers between devices: 170 us -> none  [shards(): shard_piece = lax.all_gather(rounded, ROW, axis=0, tiled=True)]
    all_to_all x0 -> x1, blocking collectives: none -> 148 us  [shards(): shard_piece = jnp.concatenate(lax.all_to_all(outgoing, ROW, 0, 0), axis=0)]
    all_to_all x0 -> x1, waiting for transfers between devices: none -> 136 us  [shards(): shard_piece = jnp.concatenate(lax.all_to_all(outgoing, ROW, 0, 0), axis=0)]
    all_to_all x0 -> x1, starting transfers between devices: none -> 8.96 us  [shards(): shard_piece = jnp.concatenate(lax.all_to_all(outgoing, ROW, 0, 0), axis=0)]
  transfers between devices with their start and end apart: 5 -> 4, of which waited for: 5 -> 4; matrix products, arithmetic and copies ran while one was open for 3% -> 2% of each run, Pallas kernels for 0% -> 0%
where the time goes in v1:
time: 591 us
  waiting for transfers between devices  332 us (56%)
  blocking collectives  192 us (32%)
  matrix products  20.7 us (4%)
  local copies, waits for them, and re-layouts  15 us (3%)
  between operations  13.9 us (2%)
  starting transfers between devices  9.08 us (2%)
  other arithmetic  7.76 us (1%)
    reduce_scatter x2, waiting for transfers between devices, sum_by_axis(): so_far = lax.psum_scatter(so_far, axis, scatter_dimension=0, tiled=True)  161 us
    all_to_all x1, blocking collectives, shards(): shard_piece = jnp.concatenate(lax.all_to_all(outgoing, ROW, 0, 0), axis=0)  148 us
    all_to_all x1, waiting for transfers between devices, shards(): shard_piece = jnp.concatenate(lax.all_to_all(outgoing, ROW, 0, 0), axis=0)  136 us
    all_to_all x2, blocking collectives, sent_to_all(): return lax.all_to_all(copies, axis, split_axis=0, concat_axis=0, tiled=True)  44.4 us
    all_gather x1, waiting for transfers between devices, shards(): gram_slabs = lax.all_gather(grams, 'col', axis=2, tiled=True)  35.5 us
  transfers between devices with their start and end apart: 4, of which 4 were waited for; matrix products, arithmetic and copies ran while one was open for 2% of the time, Pallas kernels for 0%

profile of v1, /device:TPU:32, one launch (start us, length us, event | category | flops | bytes accessed | tf_op | source)
XLA Modules:
  0.0 590.8 jit_solution(7656078979529393374)
XLA Ops:
  7.2 0.0 all-gather.2.cloned.1.call-start
  7.2 2.1 copy.14
  9.3 0.0 all-gather.2.cloned.1.call-update
  9.3 0.0 reduce-scatter.3.cloned.1.call-start
  9.4 35.5 %all-gather.2.cloned.1.call-done = bf16[4,112,3584]{1,2,0:T(8,128)(2,1)} async-done(((bf16[4,112,448]{1,2,0:T(8,128)(2,1)}), bf16[4,112,3584]{1,2,0:T(8,128)(2,1)}) %all-gather.2.cloned.1.call-update) | async-done | bytes 3211280 | tf_op jit(solution)/shard_map/all_gather | solution.py:40
  44.9 8.9 %convolution_bitcast_fusion = f32[3584,896]{1,0:T(8,128)} fusion(bf16[4,112,3584]{1,2,0:T(8,128)(2,1)} %all-gather.2.cloned.1.call-done, bf16[4,112,896]{2,1,0:T(8,128)(2,1)S(1)} %copy-done), kind=kOutput, calls=%fused_computation.2 | convolution fusion | flops 2877292544 | bytes 16859136 | tf_op jit(solution)/shard_map/mrk,mrc->kc/dot_general | solution.py:49
  53.8 0.0 reduce-scatter.5.cloned.1.call-start
  53.8 119.3 %reduce-scatter.3.cloned.1.call-done = f32[896,896]{1,0:T(8,128)} async-done(((f32[3584,896]{1,0:T(8,128)}), f32[896,896]{1,0:T(8,128)}) %reduce-scatter.3.cloned.1.call-update) | async-done | bytes 3211280 | tf_op jit(solution)/shard_map/reduce_scatter | solution.py:13
  173.1 0.9 constant_dynamic-slice_fusion.1
  174.0 3.2 copy.15
  177.3 2.9 gather_fusion
  180.2 0.6 fusion.2
  180.8 41.3 %reduce-scatter.5.cloned.1.call-done = f32[112,896]{1,0:T(8,128)} async-done(((f32[896,896]{1,0:T(8,128)}), f32[112,896]{1,0:T(8,128)}) %reduce-scatter.5.cloned.1.call-update) | async-done | bytes 401424 | tf_op jit(solution)/shard_map/reduce_scatter | solution.py:13
  222.1 1.1 fusion.10
  223.2 3.2 stack.4
  226.3 9.0 %all-to-all-start = ((bf16[32,112,896]{2,1,0:T(8,128)(2,1)}), bf16[32,112,896]{2,1,0:T(8,128)(2,1)}, u32[]{:S(2)}, u32[]{:S(2)}) async-start(bf16[32,112,896]{2,1,0:T(8,128)(2,1)} %stack.4), calls=%async_computation.2 | async-start | bytes 12845056 | tf_op jit(solution)/shard_map/all_to_all | solution.py:59
  235.3 3.0 convert_reduce_fusion
  238.4 0.1 copy.24
  238.5 1.7 gather_fusion.1
  240.2 136.0 %all-to-all-done = bf16[32,112,896]{2,1,0:T(8,128)(2,1)} async-done(((bf16[32,112,896]{2,1,0:T(8,128)(2,1)}), bf16[32,112,896]{2,1,0:T(8,128)(2,1)}, u32[]{:S(2)}, u32[]{:S(2)}) %all-to-all-start) | async-done | bytes 6422560 | tf_op jit(solution)/shard_map/all_to_all | solution.py:59
  376.1 6.9 %multiply_reduce_fusion.6 = (f32[896]{0:T(1024)S(1)}, f32[896]{0:T(1024)S(1)}, f32[896]{0:T(1024)S(1)}, f32[112,896]{1,0:T(8,128)}) fusion(f32[112,896]{1,0:T(8,128)S(1)} %get-tuple-element.14, bf16[112,896]{1,0:T(8,128)(2,1)S(1)} %get-tuple-element.13, f32[112]{0:T(128)S(1)} %broadcast_multiply_fusion, f32[112,3584]{0,1:T(8,128)S(1)} %convert_reduce_fusion, ...), kind=kOutput, calls=%fused_computation.22 | convolution fusion | flops 4316939776 | bytes 9042880 | tf_op jit(solution)/shard_map/dot_general | solution.py:61
  383.1 0.2 broadcast_in_dim.12
  383.3 24.7 %all_to_all.22 = f32[32,1,3584]{2,1,0:T(1,128)S(1)} all-to-all(f32[32,1,3584]{2,1,0:T(1,128)S(1)} %broadcast_in_dim.12), channel_id=1, replica_groups=mesh['row_0'=4,'row_1'=8,'col'=8] {'row_0','row_1'}, dimensions={0} | all-to-all | bytes 917504 | tf_op jit(solution)/shard_map/all_to_all | solution.py:19
  408.1 0.3 reduce_sum.98
  408.4 1.1 fusion.5
  409.4 0.5 stack.5
  409.9 147.9 %all_to_all.23 = bf16[32,112,896]{2,1,0:T(8,128)(2,1)S(1)} all-to-all(bf16[32,112,896]{2,1,0:T(8,128)(2,1)S(1)} %stack.5), channel_id=1, replica_groups=mesh['row_0'=4,'row_1'=8,'col'=8] {'row_0','row_1'}, dimensions={0} | all-to-all | bytes 12845056 | tf_op jit(solution)/shard_map/all_to_all | solution.py:59
  557.8 4.3 multiply_reduce_fusion.3
  562.1 0.2 broadcast_in_dim.13
  562.3 19.7 %all_to_all.24 = f32[32,1,3584]{2,1,0:T(1,128)S(1)} all-to-all(f32[32,1,3584]{2,1,0:T(1,128)S(1)} %broadcast_in_dim.13), channel_id=1, replica_groups=mesh['row_0'=4,'row_1'=8,'col'=8] {'row_0','row_1'}, dimensions={0} | all-to-all | bytes 917504 | tf_op jit(solution)/shard_map/all_to_all | solution.py:19
  582.0 0.3 reduce_sum.103
  582.3 2.0 multiply_subtract_fusion
  (11 shorter events, 0.1 us)
Async XLA Ops:
  7.2 37.7 %copy-start = (bf16[4,112,896]{2,1,0:T(8,128)(2,1)S(1)}, bf16[4,112,896]{2,1,0:T(8,128)(2,1)}, u32[]{:S(2)}) copy-start(bf16[4,112,896]{2,1,0:T(8,128)(2,1)} %param.3) | copy-start | bytes 2408452
  7.2 37.7 %all-gather.2.cloned.1.call-start = ((), (), s32[]{:S(2)}) async-start(), calls=%async_computation.6 | async-start | bytes 4128768 | tf_op jit(solution)/shard_map/all_gather | solution.py:40
  9.3 163.8 %reduce-scatter.3.cloned.1.call-start = ((), (), s32[]{:S(2)}) async-start(), calls=%async_computation.7 | async-start | bytes 16056320 | tf_op jit(solution)/shard_map/reduce_scatter | solution.py:13
  53.8 168.3 %reduce-scatter.5.cloned.1.call-start = ((), (), s32[]{:S(2)}) async-start(), calls=%async_computation.8 | async-start | bytes 3612672 | tf_op jit(solution)/shard_map/reduce_scatter | solution.py:13
  226.3 149.8 %all-to-all-start = ((bf16[32,112,896]{2,1,0:T(8,128)(2,1)}), bf16[32,112,896]{2,1,0:T(8,128)(2,1)}, u32[]{:S(2)}, u32[]{:S(2)}) async-start(bf16[32,112,896]{2,1,0:T(8,128)(2,1)} %stack.4), calls=%async_computation.2 | async-start | bytes 12845056 | tf_op jit(solution)/shard_map/all_to_all | solution.py:59
Sparse Core Ops, SparseCore 0:
  9.8 34.9 all-gather.1
  53.9 119.1 reduce-scatter.2
  175.6 46.4 reduce-scatter.4
